TPU v7x, 32 devices: a whole 2x2x4 slice. The times are simulated.
32 devices in a mesh: row: 8 (over z, x), col: 4 (over y, core).
Axes of the slice: x: 2, y: 2, z: 4, core: 2. Of those that a mesh axis runs over, the one named last changes fastest.
Arguments:
- embedding: float32 [8192, 128], P(('row', 'col')), may hold values from -6 to 6
- degrees: int32 [8192], P(('row', 'col')), may hold values from 16 to 64
- tile_values: bfloat16 [8, 4, 128, 256, 256], P('row', 'col'), may hold values from -0.1796875 to 0.1796875
- tile_layout: int32 [8, 4, 128, 2], P('row', 'col'), may hold values from 0 to 7, as said below
- tile_count: int32 [8, 4], P('row', 'col'), may hold values from 16 to 128, as said below
- coefficients: float32 [7], replicated, may hold values from -1 to 1
Outputs:
- filtered: float32 [8192, 128], P(('row', 'col'))
Inputs may be any that keep to these rules, and one draw needn't show every extreme that they name: `tile_layout`: entry [r, c, s, 0] is a row block below 8 and entry [r, c, s, 1] a column block below 4; entries of slots at or past tile_count[r, c] are valid but unused; a place may repeat. `tile_count`: some device has all 128 slots live.
All inputs are finite; a program needn't handle non-finite values.
Results may differ from a plain program's by a relative error of at most 0.0015.
Values may be sent and summed in bfloat16 or wider, within the bound.
A program may use at most 128 MiB of HBM per device.

v0:
```python
import jax
import jax.numpy as jnp
from jax import lax
from jax.sharding import PartitionSpec as P

ORDER = 6


spectral_shift = 0.5
group_slots = 8


def slot_products(tile_block, layout_block, start_slot, stop_slot, source_blocks, row_blocks):
    block_size = tile_block.shape[1]
    feat_width = source_blocks.shape[2]
    first_group = start_slot // group_slots
    last_group = (stop_slot + group_slots - 1) // group_slots
    block_ids = lax.iota(jnp.int32, row_blocks)

    def group_step(group_num, running):
        first_slot = group_num * group_slots
        group_tiles = lax.dynamic_slice_in_dim(tile_block, first_slot, group_slots, 0)
        group_layout = lax.dynamic_slice_in_dim(layout_block, first_slot, group_slots, 0)
        picked = jnp.take(source_blocks, group_layout[:, 1], axis=0)
        products = jnp.einsum(
            "kab,kbf->kaf", group_tiles, picked, preferred_element_type=jnp.float32
        )
        slot_number = first_slot + lax.iota(jnp.int32, group_slots)
        in_range = (slot_number >= start_slot) & (slot_number < stop_slot)
        one_hot = jnp.where(
            (group_layout[:, 0][None, :] == block_ids[:, None]) & in_range[None, :], 1.0, 0.0
        ).astype(jnp.float32)
        return running + jnp.einsum(
            "rk,kaf->raf", one_hot, products, precision=lax.Precision.HIGHEST
        )

    zeros_init = jnp.zeros((row_blocks, block_size, feat_width), jnp.float32)
    return lax.fori_loop(first_group, last_group, group_step, zeros_init)


def per_device(embedding, degrees, tile_values, tile_layout, tile_count, coefficients):
    tile_block = tile_values[0, 0]
    layout_block = tile_layout[0, 0]
    live_count = tile_count[0, 0]
    block_size = tile_block.shape[1]
    piece_rows = embedding.shape[0]
    feat_width = embedding.shape[1]
    row_devices = lax.axis_size("row")
    row_blocks = row_devices * piece_rows // block_size
    inv_root = lax.rsqrt(degrees.astype(jnp.float32))[:, None]

    def operate(vector):
        scaled = (inv_root * vector).astype(jnp.bfloat16)
        gathered = lax.all_gather(scaled, "col", axis=0, tiled=True)
        source_blocks = gathered.reshape(-1, block_size, feat_width)
        partial_value = slot_products(
            tile_block, layout_block, 0, live_count, source_blocks, row_blocks
        )
        partial_value = partial_value.reshape(row_devices * piece_rows, feat_width)
        summed = lax.psum_scatter(partial_value, "row", scatter_dimension=0, tiled=True)
        return (1.0 - spectral_shift) * vector - inv_root * summed

    previous = embedding
    current = operate(embedding)
    filtered = coefficients[0] * previous + coefficients[1] * current
    for order in range(2, ORDER + 1):
        following = 2.0 * operate(current) - previous
        filtered = filtered + coefficients[order] * following
        previous, current = (current, following)
    return filtered


def solution(mesh):
    in_specs = (
        P(("row", "col"), None),
        P(("row", "col")),
        P("row", "col", None, None, None),
        P("row", "col", None, None),
        P("row", "col"),
        P(),
    )
    out_specs = P(("row", "col"), None)
    return jax.shard_map(
        per_device, mesh=mesh, in_specs=in_specs, out_specs=out_specs, check_vma=False
    )
```

profile of v0, /device:TPU:0, one launch (start us, length us, event | category | flops | bytes accessed | tf_op | source)
XLA Modules:
  0.0 988.1 jit_solution(17452015672896146708)
XLA Ops:
  8.9 7.3 all_gather.18
  16.2 28.5 %while.66 = (s32[]{:T(128)}, f32[8,256,128]{2,0,1:T(8,128)S(1)}, s32[]{:T(128)}, s32[128,2]{0,1:T(2,128)}, s32[]{:T(128)}, /*index=5*/bf16[128,256,256]{2,1,0:T(...) while((s32[]{:T(128)}, f32[8,256,128]{2,0,1:T(8,128)S(1)}, ...), condition=%wide.region_1.3_spmd.clone, body=%wide.region_0.2_spmd.clone.sunk | while | flops 159909136 | bytes 6820395 | solution.py:38
  31.5 1.8 convolution_add_fusion.12
  37.2 1.8 convolution_add_fusion.12
  42.9 1.8 convolution_add_fusion.12
  46.0 124.3 %reduce-scatter.7.cloned.1.call-done = f32[256,128]{1,0:T(8,128)} async-done(((f32[2048,128]{1,0:T(8,128)}), f32[256,128]{1,0:T(8,128)}) %reduce-scatter.7.cloned.1.call-update) | async-done | bytes 131088 | tf_op jit(solution)/shard_map/reduce_scatter | solution.py:60
  171.3 5.8 all_gather.19
  177.2 28.5 %while.67 = (s32[]{:T(128)}, f32[8,256,128]{2,0,1:T(8,128)S(1)}, s32[]{:T(128)}, s32[128,2]{0,1:T(2,128)}, s32[]{:T(128)}, /*index=5*/bf16[128,256,256]{2,1,0:T(...) while((s32[]{:T(128)}, f32[8,256,128]{2,0,1:T(8,128)S(1)}, ...), condition=%wide.region_4.6_spmd.clone, body=%wide.region_3.5_spmd.clone.sunk | while | flops 159909136 | bytes 6820395 | solution.py:38
  192.4 1.8 convolution_add_fusion.13
  203.8 1.8 convolution_add_fusion.13
  207.0 124.2 %reduce-scatter.9.cloned.1.call-done = f32[256,128]{1,0:T(8,128)} async-done(((f32[2048,128]{1,0:T(8,128)}), f32[256,128]{1,0:T(8,128)}) %reduce-scatter.9.cloned.1.call-update) | async-done | bytes 131088 | tf_op jit(solution)/shard_map/reduce_scatter | solution.py:60
  332.2 5.8 all_gather.20
  338.1 28.5 %while.68 = (s32[]{:T(128)}, f32[8,256,128]{2,0,1:T(8,128)S(1)}, s32[]{:T(128)}, s32[128,2]{0,1:T(2,128)}, s32[]{:T(128)}, /*index=5*/bf16[128,256,256]{2,1,0:T(...) while((s32[]{:T(128)}, f32[8,256,128]{2,0,1:T(8,128)S(1)}, ...), condition=%wide.region_7.9_spmd.clone, body=%wide.region_6.8_spmd.clone.sunk | while | flops 159909136 | bytes 6820395 | solution.py:38
  353.3 1.8 convolution_add_fusion.14
  364.7 1.8 convolution_add_fusion.14
  367.8 124.2 %reduce-scatter.11.cloned.1.call-done = f32[256,128]{1,0:T(8,128)} async-done(((f32[2048,128]{1,0:T(8,128)}), f32[256,128]{1,0:T(8,128)}) %reduce-scatter.11.cloned.1.call-update) | async-done | bytes 131088 | tf_op jit(solution)/shard_map/reduce_scatter | solution.py:60
  493.0 5.8 all_gather.21
  498.9 28.7 %while.69 = (s32[]{:T(128)}, f32[8,256,128]{2,0,1:T(8,128)S(1)}, s32[]{:T(128)}, s32[128,2]{0,1:T(2,128)}, s32[]{:T(128)}, /*index=5*/bf16[128,256,256]{2,1,0:T(...) while((s32[]{:T(128)}, f32[8,256,128]{2,0,1:T(8,128)S(1)}, ...), condition=%wide.region_10.12_spmd.clone, body=%wide.region_9.11_spmd.clone.sunk | while | flops 159909136 | bytes 6820395 | solution.py:38
  514.3 1.8 convolution_add_fusion.15
  525.7 1.8 convolution_add_fusion.15
  528.8 124.3 %reduce-scatter.13.cloned.1.call-done = f32[256,128]{1,0:T(8,128)} async-done(((f32[2048,128]{1,0:T(8,128)}), f32[256,128]{1,0:T(8,128)}) %reduce-scatter.13.cloned.1.call-update) | async-done | bytes 131088 | tf_op jit(solution)/shard_map/reduce_scatter | solution.py:60
  654.1 5.8 all_gather.22
  660.0 28.5 %while.70 = (s32[]{:T(128)}, f32[8,256,128]{2,0,1:T(8,128)S(1)}, s32[]{:T(128)}, s32[128,2]{0,1:T(2,128)}, s32[]{:T(128)}, /*index=5*/bf16[128,256,256]{2,1,0:T(...) while((s32[]{:T(128)}, f32[8,256,128]{2,0,1:T(8,128)S(1)}, ...), condition=%wide.region_13.15_spmd.clone, body=%wide.region_12.14_spmd.clone.sunk | while | flops 159909136 | bytes 6820395 | solution.py:38
  675.3 1.8 convolution_add_fusion.16
  686.7 1.8 convolution_add_fusion.16
  689.8 124.2 %reduce-scatter.15.cloned.1.call-done = f32[256,128]{1,0:T(8,128)} async-done(((f32[2048,128]{1,0:T(8,128)}), f32[256,128]{1,0:T(8,128)}) %reduce-scatter.15.cloned.1.call-update) | async-done | bytes 131088 | tf_op jit(solution)/shard_map/reduce_scatter | solution.py:60
  815.0 5.8 all_gather.23
  820.9 28.5 %while.71 = (s32[]{:T(128)}, f32[8,256,128]{2,0,1:T(8,128)S(1)}, s32[]{:T(128)}, s32[128,2]{0,1:T(2,128)}, s32[]{:T(128)}, /*index=5*/bf16[128,256,256]{2,1,0:T(...) while((s32[]{:T(128)}, f32[8,256,128]{2,0,1:T(8,128)S(1)}, ...), condition=%wide.region_16.18_spmd.clone, body=%wide.region_15.17_spmd.clone.sunk | while | flops 159909136 | bytes 6820395 | solution.py:38
  836.2 1.8 convolution_add_fusion.17
  847.6 1.8 convolution_add_fusion.17
  851.3 123.7 %reduce-scatter.17.cloned.1.call-done = f32[256,128]{1,0:T(8,128)} async-done(((f32[2048,128]{1,0:T(8,128)}), f32[256,128]{1,0:T(8,128)}) %reduce-scatter.17.cloned.1.call-update) | async-done | bytes 131088 | tf_op jit(solution)/shard_map/reduce_scatter | solution.py:60
  975.1 6.2 multiply_add_fusion
  (239 shorter events, 160.3 us)
Async XLA Ops:
  6.5 163.8 %reduce-scatter.7.cloned.1.call-start = ((), (), s32[]{:S(2)}) async-start(), calls=%async_computation.6 | async-start | bytes 1179648 | tf_op jit(solution)/shard_map/reduce_scatter | solution.py:60
  16.2 154.1 %copy-start = (f32[256,128]{1,0:T(8,128)S(1)}, f32[256,128]{1,0:T(8,128)}, u32[]{:S(2)}) copy-start(f32[256,128]{1,0:T(8,128)} %param.20) | copy-start | bytes 393220
  46.0 285.2 %reduce-scatter.9.cloned.1.call-start = ((), (), s32[]{:S(2)}) async-start(), calls=%async_computation.7 | async-start | bytes 1179648 | tf_op jit(solution)/shard_map/reduce_scatter | solution.py:60
  177.2 154.0 %copy-start.1 = (f32[256,128]{1,0:T(8,128)S(1)}, f32[256,128]{1,0:T(8,128)}, u32[]{:S(2)}) copy-start(f32[256,128]{1,0:T(8,128)} %reduce-scatter.7.cloned.1.call-done) | copy-start | bytes 393220
  206.9 285.1 %reduce-scatter.11.cloned.1.call-start = ((), (), s32[]{:S(2)}) async-start(), calls=%async_computation.8 | async-start | bytes 1179648 | tf_op jit(solution)/shard_map/reduce_scatter | solution.py:60
  367.8 285.3 %reduce-scatter.13.cloned.1.call-start = ((), (), s32[]{:S(2)}) async-start(), calls=%async_computation.9 | async-start | bytes 1179648 | tf_op jit(solution)/shard_map/reduce_scatter | solution.py:60
  528.8 285.2 %reduce-scatter.15.cloned.1.call-start = ((), (), s32[]{:S(2)}) async-start(), calls=%async_computation.10 | async-start | bytes 1179648 | tf_op jit(solution)/shard_map/reduce_scatter | solution.py:60
  660.0 154.0 %copy-start.2 = (f32[256,128]{1,0:T(8,128)S(1)}, f32[256,128]{1,0:T(8,128)}, u32[]{:S(2)}) copy-start(f32[256,128]{1,0:T(8,128)} %reduce-scatter.13.cloned.1.call-done) | copy-start | bytes 393220
  689.7 285.3 %reduce-scatter.17.cloned.1.call-start = ((), (), s32[]{:S(2)}) async-start(), calls=%async_computation.11 | async-start | bytes 1179648 | tf_op jit(solution)/shard_map/reduce_scatter | solution.py:60
  820.9 29.8 %copy-start.4 = (f32[7]{0:T(128)S(1)}, f32[7]{0:T(128)}, u32[]{:S(2)}) copy-start(f32[7]{0:T(128)} %param.25) | copy-start | bytes 88
  820.9 154.2 %copy-start.3 = (f32[256,128]{1,0:T(8,128)S(1)}, f32[256,128]{1,0:T(8,128)}, u32[]{:S(2)}) copy-start(f32[256,128]{1,0:T(8,128)} %reduce-scatter.15.cloned.1.call-done) | copy-start | bytes 393220
Sparse Core Ops, SparseCore 0:
  46.1 124.1 reduce-scatter.6
  207.0 124.1 reduce-scatter.8
  367.9 124.0 reduce-scatter.10
  528.9 124.1 reduce-scatter.12
  689.9 124.0 reduce-scatter.14
  850.8 124.2 reduce-scatter.16
where the time goes:
time: 1000 us; the launch traced here: 988 us
  waiting for transfers between devices  745 us (74%)
  matrix products  107 us (11%)
  local copies, waits for them, and re-layouts  50.5 us (5%)
  blocking collectives  36.1 us (4%)
  other arithmetic  32.7 us (3%)
  between operations  14.3 us (1%)
    reduce_scatter x6, waiting for transfers between devices, operate(): lax.psum_scatter(partial_value, 'row', scatter_dimension=0, tiled=True)  745 us
    dot_general x30, matrix products, group_step(): jnp.einsum('rk,kaf->raf', one_hot, products, precision=lax.Precision.HIGH...  55.3 us
    dot_general x30, matrix products, group_step(): jnp.einsum('kab,kbf->kaf', group_tiles, picked, preferred_element_type=jn...  51.7 us
    all_gather x6, blocking collectives, operate(): gathered = lax.all_gather(scaled, 'col', axis=0, tiled=True)  36.1 us
    dynamic_slice x30, local copies, waits for them, and re-layouts, group_step(): lax.dynamic_slice_in_dim(layout_block, first_slot, group_slots, 0)  22.8 us
  transfers between devices with their start and end apart: 6, of which 6 were waited for; matrix products, arithmetic and copies ran while one was open for 0% of the time, Pallas kernels for 0%

commit v1 on v0

v1 whole, which is shorter than its diff:
```python
import functools

import jax
import jax.numpy as jnp
from jax import lax
from jax.experimental import pallas as pl
from jax.experimental.pallas import tpu as pltpu
from jax.sharding import PartitionSpec as P

ORDER = 6
SHIFT = 0.5
CHUNK = 4
DEPTH = 8
MESH = pl.DeviceIdType.MESH
VMEM_LIMIT = 60 * 1024 * 1024


def merge_kernel(n_row, n_col, count_ref, layout_ref, tiles_ref, hi_ref, lo_ref,
                 total, landed, stage, in_sem, out_sem):
    block = tiles_ref.shape[1]
    count = count_ref[0]
    chunks = (count + CHUNK - 1) // CHUNK

    def fetch(chunk):
        slot = lax.rem(chunk, DEPTH)
        return pltpu.make_async_copy(
            tiles_ref.at[pl.ds(chunk * CHUNK, CHUNK)], landed.at[slot], in_sem.at[slot])

    for ahead in range(DEPTH):
        @pl.when(ahead < chunks)
        def _():
            fetch(jnp.int32(ahead)).start()

    def clear(place, carry):
        total[place] = jnp.zeros((block, block), jnp.float32)
        return carry

    lax.fori_loop(0, n_row * n_col, clear, 0)

    def add_chunk(chunk, carry):
        slot = lax.rem(chunk, DEPTH)
        fetch(chunk).wait()
        for inner in range(CHUNK):
            number = chunk * CHUNK + inner

            @pl.when(number < count)
            def _():
                place = layout_ref[2 * number] * n_col + layout_ref[2 * number + 1]
                total[place] += landed[slot, inner].astype(jnp.float32)

        @pl.when(chunk + DEPTH < chunks)
        def _():
            fetch(chunk + DEPTH).start()
        return carry

    lax.fori_loop(0, chunks, add_chunk, 0)

    def outgoing(row):
        slot = lax.rem(row, 2)
        return (pltpu.make_async_copy(stage.at[slot, 0], hi_ref.at[row], out_sem.at[slot, 0]),
                pltpu.make_async_copy(stage.at[slot, 1], lo_ref.at[row], out_sem.at[slot, 1]))

    def put_row(row, carry):
        slot = lax.rem(row, 2)

        @pl.when(row >= 2)
        def _():
            for copy in outgoing(row - 2):
                copy.wait()
        for col in range(n_col):
            value = total[row * n_col + col]
            high = value.astype(jnp.bfloat16)
            stage[slot, 0, :, col * block:(col + 1) * block] = high
            stage[slot, 1, :, col * block:(col + 1) * block] = (
                value - high.astype(jnp.float32)).astype(jnp.bfloat16)
        for copy in outgoing(row):
            copy.start()
        return carry

    lax.fori_loop(0, n_row, put_row, 0)
    for row in (n_row - 2, n_row - 1):
        for copy in outgoing(jnp.int32(row)):
            copy.wait()


def filter_kernel(nz, nx, nc, coef_ref, emb_ref, inv_ref, hi_ref, lo_ref, out_ref,
                  prev, cur, field, part_a, part_b, rx_a, rx_b, zr_a, zr_b,
                  ag_send, ag_recv, xa_send, xa_recv, za_send, za_recv,
                  zb_send, zb_recv, xb_send, xb_recv):
    r = lax.axis_index("row")
    c = lax.axis_index("col")
    z, x = r // nx, lax.rem(r, nx)
    piece = emb_ref.shape[0]
    half = piece // 2

    def rows_of(owner, part):
        return pl.ds(pl.multiple_of(owner * piece + part * half, half), half)

    def remote(src, dst, send_sem, recv_sem, **where):
        return pltpu.make_async_remote_copy(
            src_ref=src, dst_ref=dst, send_sem=send_sem, recv_sem=recv_sem,
            device_id={"row": where.get("row", r), "col": where.get("col", c)},
            device_id_type=MESH)

    def gather_copy(p, part, offset, owner):
        spot = field.at[p, rows_of(owner, part)]
        return remote(spot, spot, ag_send.at[part, offset], ag_recv.at[p, part, owner],
                      col=lax.rem(c + offset, nc))

    def cross_a(p, d, other, source):
        return remote(part_a.at[d, other], rx_a.at[p, d, source],
                      xa_send.at[d, other], xa_recv.at[p, d, source], row=z * nx + other)

    def cross_b(p, other, source):
        return remote(part_b.at[z, other], rx_b.at[p, source],
                      xb_send.at[other], xb_recv.at[p, source], row=z * nx + other)

    def line_a(p, way, d, neighbour):
        return remote(part_a.at[d, x], zr_a.at[p, way, d],
                      za_send.at[d], za_recv.at[p, way, d], row=neighbour * nx + x)

    def line_b(p, way, d, neighbour):
        return remote(part_b.at[d], zr_b.at[p, way, d],
                      zb_send.at[d], zb_recv.at[p, way, d], row=neighbour * nx + x)

    def visit(t):
        d = jnp.where(2 * z >= nz, t, nz - 1 - t)
        upward = d > z
        way = jnp.where(upward, 0, 1)
        neighbour = jnp.clip(jnp.where(upward, z + 1, z - 1), 0, nz - 1)
        first = jnp.where(upward, z == 0, z == nz - 1)
        return d, way, neighbour, first

    others = [lax.rem(x + 1 + u, nx) for u in range(nx - 1)]

    def share(p, part, value):
        field[p, rows_of(c, part)] = value.astype(jnp.bfloat16)
        for offset in range(1, nc):
            gather_copy(p, part, offset, c).start()

    barrier = pltpu.get_barrier_semaphore()
    for other in others:
        pl.semaphore_signal(barrier, inc=1, device_id={"row": z * nx + other, "col": c},
                            device_id_type=MESH)
    for offset in range(1, nc):
        pl.semaphore_signal(barrier, inc=1, device_id={"row": r, "col": lax.rem(c + offset, nc)},
                            device_id_type=MESH)

    @pl.when(z > 0)
    def _():
        pl.semaphore_signal(barrier, inc=1, device_id={"row": r - nx, "col": c},
                            device_id_type=MESH)

    @pl.when(z < nz - 1)
    def _():
        pl.semaphore_signal(barrier, inc=1, device_id={"row": r + nx, "col": c},
                            device_id_type=MESH)
    pl.semaphore_wait(barrier, nx - 1 + nc - 1 + jnp.where(z > 0, 1, 0)
                      + jnp.where(z < nz - 1, 1, 0))

    start = emb_ref[...]
    prev[...] = start
    cur[...] = start
    out_ref[...] = coef_ref[0] * start
    for part in range(2):
        span = slice(part * half, (part + 1) * half)
        share(0, part, inv_ref[span] * emb_ref[span])

    def step(k, carry):
        p = lax.rem(k, 2)
        for offset in range(1, nc):
            for part in range(2):
                copy = gather_copy(p, part, offset, lax.rem(c + offset, nc))
                copy.wait_send()
                copy.wait_recv()

        def multiply(t, inner):
            d, way, neighbour, first = visit(t)
            for u in range(nx):
                other = lax.rem(x + 1 + u, nx)
                number = d * nx + other
                source = field[p]
                value = (jnp.dot(hi_ref[number], source, preferred_element_type=jnp.float32)
                         + jnp.dot(lo_ref[number], source, preferred_element_type=jnp.float32))
                part_a[d, other] = value[:half]
                part_b[d, other] = value[half:]
                if u < nx - 1:
                    cross_a(p, d, other, x).start()

            @pl.when((d != z) & first)
            def _():
                line_b(p, way, d, neighbour).start()
            return inner

        lax.fori_loop(0, nz, multiply, 0)

        def collect_a(d):
            for other in others:
                cross_a(p, d, other, other).wait_recv()
                part_a[d, x] += rx_a[p, d, other]

        def pass_on(t, inner):
            d, way, neighbour, first = visit(t)

            @pl.when((d != z) & jnp.logical_not(first))
            def _():
                line_b(p, way, d, neighbour).wait_recv()
                part_b[d] += zr_b[p, way, d]
                line_b(p, way, d, neighbour).start()

            @pl.when(d != z)
            def _():
                collect_a(d)

                @pl.when(jnp.logical_not(first))
                def _():
                    line_a(p, way, d, neighbour).wait_recv()
                    part_a[d, x] += zr_a[p, way, d]
                line_a(p, way, d, neighbour).start()
            return inner

        lax.fori_loop(0, nz, pass_on, 0)

        arrivals = ((0, z > 0), (1, z < nz - 1))
        for way, there in arrivals:
            @pl.when(there)
            def _():
                line_b(p, way, z, z).wait_recv()
                part_b[z] += zr_b[p, way, z]
        for other in others:
            cross_b(p, other, x).start()
        collect_a(z)
        for way, there in arrivals:
            @pl.when(there)
            def _():
                line_a(p, way, z, z).wait_recv()
                part_a[z, x] += zr_a[p, way, z]

        alpha = jnp.where(k == 0, 1.0, 2.0).astype(jnp.float32)
        beta = jnp.where(k == 0, 0.0, 1.0).astype(jnp.float32)
        weight = coef_ref[k + 1]

        def finish(part, summed):
            span = slice(part * half, (part + 1) * half)
            now = cur[span]
            moved = (1.0 - SHIFT) * now - inv_ref[span] * summed
            following = alpha * moved - beta * prev[span]
            prev[span] = now
            cur[span] = following
            out_ref[span] = out_ref[span] + weight * following

            @pl.when(k < ORDER - 1)
            def _():
                share(1 - p, part, inv_ref[span] * following)

        finish(0, part_a[z, x])
        summed = part_b[z, x]
        for other in others:
            cross_b(p, other, other).wait_recv()
            summed = summed + rx_b[p, other]
        finish(1, summed)

        for other in others:
            cross_b(p, other, x).wait_send()

        def drain(t, inner):
            d, way, neighbour, first = visit(t)
            for other in others:
                cross_a(p, d, other, x).wait_send()

            @pl.when(d != z)
            def _():
                line_a(p, way, d, neighbour).wait_send()
                line_b(p, way, d, neighbour).wait_send()
            return inner

        lax.fori_loop(0, nz, drain, 0)
        return carry

    lax.fori_loop(0, ORDER, step, 0)


def grid_of(n):
    nx = 1
    while nx * nx * 4 <= n and n % (nx * 2) == 0:
        nx *= 2
    return n // nx, nx


def solution(mesh):
    n_row, n_col = mesh.shape["row"], mesh.shape["col"]
    nz, nx = grid_of(n_row)

    def per_device(embedding, degrees, tile_values, tile_layout, tile_count, coefficients):
        tiles = tile_values[0, 0]
        block = tiles.shape[1]
        piece, width = embedding.shape
        half = piece // 2
        inv = lax.rsqrt(degrees.astype(jnp.float32))[:, None]
        inv = jnp.broadcast_to(inv, (piece, width))
        smem = pl.BlockSpec(memory_space=pltpu.SMEM)
        vmem = pl.BlockSpec(memory_space=pltpu.VMEM)
        anywhere = pl.BlockSpec(memory_space=pl.ANY)
        weight = jax.ShapeDtypeStruct((n_row, block, n_col * block), jnp.bfloat16)
        high, low = pl.pallas_call(
            functools.partial(merge_kernel, n_row, n_col),
            out_shape=(weight, weight),
            in_specs=[smem, smem, anywhere],
            out_specs=(anywhere, anywhere),
            scratch_shapes=[
                pltpu.VMEM((n_row * n_col, block, block), jnp.float32),
                pltpu.VMEM((DEPTH, CHUNK, block, block), jnp.bfloat16),
                pltpu.VMEM((2, 2, block, n_col * block), jnp.bfloat16),
                pltpu.SemaphoreType.DMA((DEPTH,)),
                pltpu.SemaphoreType.DMA((2, 2)),
            ],
            compiler_params=pltpu.CompilerParams(vmem_limit_bytes=VMEM_LIMIT),
        )(tile_count.reshape(1), tile_layout.reshape(-1), tiles)
        dma = pltpu.SemaphoreType.DMA
        f32 = jnp.float32
        return pl.pallas_call(
            functools.partial(filter_kernel, nz, nx, n_col),
            out_shape=jax.ShapeDtypeStruct((piece, width), f32),
            in_specs=[smem, vmem, vmem, vmem, vmem],
            out_specs=vmem,
            scratch_shapes=[
                pltpu.VMEM((piece, width), f32),
                pltpu.VMEM((piece, width), f32),
                pltpu.VMEM((2, n_col * piece, width), jnp.bfloat16),
                pltpu.VMEM((nz, nx, half, width), f32),
                pltpu.VMEM((nz, nx, half, width), f32),
                pltpu.VMEM((2, nz, nx, half, width), f32),
                pltpu.VMEM((2, nx, half, width), f32),
                pltpu.VMEM((2, 2, nz, half, width), f32),
                pltpu.VMEM((2, 2, nz, nx, half, width), f32),
                dma((2, n_col)), dma((2, 2, n_col)),
                dma((nz, nx)), dma((2, nz, nx)),
                dma((nz,)), dma((2, 2, nz)),
                dma((nz,)), dma((2, 2, nz)),
                dma((nx,)), dma((2, nx)),
            ],
            compiler_params=pltpu.CompilerParams(
                collective_id=0, has_side_effects=True, vmem_limit_bytes=VMEM_LIMIT),
        )(coefficients, embedding, inv, high, low)

    return jax.shard_map(
        per_device, mesh=mesh,
        in_specs=(P(("row", "col"), None), P(("row", "col")),
                  P("row", "col", None, None, None), P("row", "col", None, None),
                  P("row", "col"), P()),
        out_specs=P(("row", "col"), None), check_vma=False)
```

time: 1000 us -> 179 us (0.18); the launches traced: 988 us -> 180 us
  waiting for transfers between devices: 745 us -> 0 us
  Pallas kernels: 0 us -> 175 us
  matrix products: 107 us -> 0 us
  local copies, waits for them, and re-layouts: 50.5 us -> 3.78 us
  blocking collectives: 36.1 us -> 0 us
  other arithmetic: 32.7 us -> 0.68 us
  between operations: 14.3 us -> 0.67 us
    reduce_scatter x6 -> x0, waiting for transfers between devices: 745 us -> none  [operate(): lax.psum_scatter(partial_value, 'row', scatter_dimension=0, tiled=True)]
    pallas_call x0 -> x2, Pallas kernels: none -> 175 us  [the longest x1 167 us: per_device(): pl.pallas_call(functools.partial(filter_kernel, nz, nx, n_col), out_shape...]
    dot_general x60 -> x0, matrix products: 107 us -> none  [the longest x30 55.3 us: group_step(): jnp.einsum('rk,kaf->raf', one_hot, products, precision=lax.Precision.HIGH...]
    all_gather x6 -> x0, blocking collectives: 36.1 us -> none  [operate(): gathered = lax.all_gather(scaled, 'col', axis=0, tiled=True)]
    dynamic_slice x30 -> x0, local copies, waits for them, and re-layouts: 22.8 us -> none  [group_step(): lax.dynamic_slice_in_dim(layout_block, first_slot, group_slots, 0)]
    and x30 -> x0, other arithmetic: 19.6 us -> none  [group_step(): picked = jnp.take(source_blocks, group_layout[:, 1], axis=0)]
    gather x30 -> x0, local copies, waits for them, and re-layouts: 19.4 us -> none  [group_step(): picked = jnp.take(source_blocks, group_layout[:, 1], axis=0)]
  transfers between devices with their start and end apart: 6 -> 0, of which waited for: 6 -> 0; matrix products, arithmetic and copies ran while one was open for 0% -> 0% of each run, Pallas kernels for 0% -> 0%
where the time goes in v1:
time: 179 us; the launch traced here: 180 us
  Pallas kernels  175 us (98%)
  local copies, waits for them, and re-layouts  3.78 us (2%)
    pallas_call x1, Pallas kernels, per_device(): pl.pallas_call(functools.partial(filter_kernel, nz, nx, n_col), out_shape...  167 us
    pallas_call x1, Pallas kernels, per_device(): pl.pallas_call(functools.partial(merge_kernel, n_row, n_col), out_shape=(...  7.66 us

profile of v1, /device:TPU:0, one launch (start us, length us, event | category | flops | bytes accessed | tf_op | source)
XLA Modules:
  0.0 180.1 jit_solution(4137013216162095389)
XLA Ops:
  0.7 0.7 convert_rsqrt_fusion
  1.3 0.8 copy.7
  2.1 0.7 reshape.8.layout_ref
  2.8 0.8 broadcast_in_dim.2.inv_ref
  3.5 7.7 %shard_map.64 = (bf16[8,256,1024]{2,1,0:T(8,128)(2,1)}, bf16[8,256,1024]{2,1,0:T(8,128)(2,1)}) custom-call(s32[1]{0:T(128)} %bitcast.4.count_ref, s32[256]{0:T(256)} %reshape.8.layout_ref, bf16[128,256,256]{2,1,0:T(8,128)(2,1)} %bitcast.5), custom_call_target="tpu_custom_call" | custom-call | tf_op jit(solution)/shard_map/pallas_call | solution.py:305
  11.2 167.3 %shard_map.65 = f32[256,128]{1,0:T(8,128)} custom-call(f32[7]{0:T(128)} %coef_ref.1, f32[256,128]{1,0:T(8,128)} %emb_ref.1, f32[256,128]{1,0:T(8,128)} %broadcast_in_dim.2.inv_ref, bf16[8,256,1024]{2,1,0:T(8,128)(2,1)} %get-tuple-element.7.hi_ref, bf16[8,256,1024]{2,1,0:T(8,128)(2,1)} %get-tuple-element.8.lo_ref), custom_call_target="tpu_custom_call" | custom-call | tf_op jit(solution)/shard_map/pallas_call | solution.py:321
  178.5 1.6 copy.10

commit v2 on v1

--- a/solution.py
+++ b/solution.py
@@ -11,6 +11,7 @@
 SHIFT = 0.5
 CHUNK = 4
 DEPTH = 8
+PIECES = 2
 MESH = pl.DeviceIdType.MESH
 VMEM_LIMIT = 60 * 1024 * 1024
 
@@ -84,14 +85,15 @@
 
 
 def filter_kernel(nz, nx, nc, coef_ref, emb_ref, inv_ref, hi_ref, lo_ref, out_ref,
-                  prev, cur, field, part_a, part_b, rx_a, rx_b, zr_a, zr_b,
-                  ag_send, ag_recv, xa_send, xa_recv, za_send, za_recv,
+                  weights, prev, cur, field, part_a, part_b, tx_a, tx_b, rx_a, rx_b, zr_a, zr_b,
+                  w_sem, ag_send, ag_recv, xa_send, xa_recv, za_send, za_recv,
                   zb_send, zb_recv, xb_send, xb_recv):
     r = lax.axis_index("row")
     c = lax.axis_index("col")
     z, x = r // nx, lax.rem(r, nx)
     piece = emb_ref.shape[0]
     half = piece // 2
+    quarter = half // PIECES
 
     def rows_of(owner, part):
         return pl.ds(pl.multiple_of(owner * piece + part * half, half), half)
@@ -108,20 +110,25 @@
                       col=lax.rem(c + offset, nc))
 
     def cross_a(p, d, other, source):
-        return remote(part_a.at[d, other], rx_a.at[p, d, source],
+        return remote(tx_a.at[d, other], rx_a.at[p, d, source],
                       xa_send.at[d, other], xa_recv.at[p, d, source], row=z * nx + other)
 
     def cross_b(p, other, source):
-        return remote(part_b.at[z, other], rx_b.at[p, source],
+        return remote(part_b.at[other], rx_b.at[p, source],
                       xb_send.at[other], xb_recv.at[p, source], row=z * nx + other)
 
-    def line_a(p, way, d, neighbour):
-        return remote(part_a.at[d, x], zr_a.at[p, way, d],
-                      za_send.at[d], za_recv.at[p, way, d], row=neighbour * nx + x)
-
-    def line_b(p, way, d, neighbour):
-        return remote(part_b.at[d], zr_b.at[p, way, d],
-                      zb_send.at[d], zb_recv.at[p, way, d], row=neighbour * nx + x)
+    def line_a(p, way, d, q, neighbour):
+        rows = pl.ds(q * quarter, quarter)
+        return remote(part_a.at[d, rows], zr_a.at[p, way, d, rows],
+                      za_send.at[d, q], za_recv.at[p, way, d, q], row=neighbour * nx + x)
+
+    def line_b(p, d, source):
+        return remote(tx_b.at[d], zr_b.at[p, source],
+                      zb_send.at[d], zb_recv.at[p, source], row=d * nx + x)
+
+    def weight_copies(number):
+        return (pltpu.make_async_copy(hi_ref.at[number], weights.at[0, number], w_sem.at[0, number]),
+                pltpu.make_async_copy(lo_ref.at[number], weights.at[1, number], w_sem.at[1, number]))
 
     def visit(t):
         d = jnp.where(2 * z >= nz, t, nz - 1 - t)
@@ -132,36 +139,36 @@
         return d, way, neighbour, first
 
     others = [lax.rem(x + 1 + u, nx) for u in range(nx - 1)]
+    levels = [lax.rem(z + 1 + u, nz) for u in range(nz - 1)]
 
     def share(p, part, value):
         field[p, rows_of(c, part)] = value.astype(jnp.bfloat16)
         for offset in range(1, nc):
             gather_copy(p, part, offset, c).start()
 
+    def load(t, carry):
+        d = visit(t)[0]
+        for u in range(nx):
+            for copy in weight_copies(d * nx + lax.rem(x + 1 + u, nx)):
+                copy.start()
+        return carry
+
     barrier = pltpu.get_barrier_semaphore()
     for other in others:
         pl.semaphore_signal(barrier, inc=1, device_id={"row": z * nx + other, "col": c},
                             device_id_type=MESH)
+    for level in levels:
+        pl.semaphore_signal(barrier, inc=1, device_id={"row": level * nx + x, "col": c},
+                            device_id_type=MESH)
     for offset in range(1, nc):
         pl.semaphore_signal(barrier, inc=1, device_id={"row": r, "col": lax.rem(c + offset, nc)},
                             device_id_type=MESH)
-
-    @pl.when(z > 0)
-    def _():
-        pl.semaphore_signal(barrier, inc=1, device_id={"row": r - nx, "col": c},
-                            device_id_type=MESH)
-
-    @pl.when(z < nz - 1)
-    def _():
-        pl.semaphore_signal(barrier, inc=1, device_id={"row": r + nx, "col": c},
-                            device_id_type=MESH)
-    pl.semaphore_wait(barrier, nx - 1 + nc - 1 + jnp.where(z > 0, 1, 0)
-                      + jnp.where(z < nz - 1, 1, 0))
-
+    lax.fori_loop(0, nz, load, 0)
     start = emb_ref[...]
     prev[...] = start
     cur[...] = start
     out_ref[...] = coef_ref[0] * start
+    pl.semaphore_wait(barrier, nx - 1 + nz - 1 + nc - 1)
     for part in range(2):
         span = slice(part * half, (part + 1) * half)
         share(0, part, inv_ref[span] * emb_ref[span])
@@ -175,21 +182,35 @@
                 copy.wait_recv()
 
         def multiply(t, inner):
-            d, way, neighbour, first = visit(t)
+            d = visit(t)[0]
             for u in range(nx):
                 other = lax.rem(x + 1 + u, nx)
                 number = d * nx + other
+
+                @pl.when(k == 0)
+                def _():
+                    for copy in weight_copies(number):
+                        copy.wait()
                 source = field[p]
-                value = (jnp.dot(hi_ref[number], source, preferred_element_type=jnp.float32)
-                         + jnp.dot(lo_ref[number], source, preferred_element_type=jnp.float32))
-                part_a[d, other] = value[:half]
-                part_b[d, other] = value[half:]
+                value = (jnp.dot(weights[0, number], source, preferred_element_type=jnp.float32)
+                         + jnp.dot(weights[1, number], source, preferred_element_type=jnp.float32))
                 if u < nx - 1:
+                    tx_a[d, other] = value[:half].astype(jnp.bfloat16)
                     cross_a(p, d, other, x).start()
-
-            @pl.when((d != z) & first)
-            def _():
-                line_b(p, way, d, neighbour).start()
+                else:
+                    part_a[d] = value[:half]
+
+                @pl.when(d == z)
+                def _():
+                    part_b[other] = value[half:]
+
+                @pl.when(d != z)
+                def _():
+                    tx_b[d, other] = value[half:].astype(jnp.bfloat16)
+
+            @pl.when(d != z)
+            def _():
+                line_b(p, d, z).start()
             return inner
 
         lax.fori_loop(0, nz, multiply, 0)
@@ -197,44 +218,32 @@
         def collect_a(d):
             for other in others:
                 cross_a(p, d, other, other).wait_recv()
-                part_a[d, x] += rx_a[p, d, other]
+                part_a[d] += rx_a[p, d, other].astype(jnp.float32)
 
         def pass_on(t, inner):
             d, way, neighbour, first = visit(t)
 
-            @pl.when((d != z) & jnp.logical_not(first))
-            def _():
-                line_b(p, way, d, neighbour).wait_recv()
-                part_b[d] += zr_b[p, way, d]
-                line_b(p, way, d, neighbour).start()
-
             @pl.when(d != z)
             def _():
                 collect_a(d)
-
-                @pl.when(jnp.logical_not(first))
-                def _():
-                    line_a(p, way, d, neighbour).wait_recv()
-                    part_a[d, x] += zr_a[p, way, d]
-                line_a(p, way, d, neighbour).start()
+                for q in range(PIECES):
+                    rows = pl.ds(q * quarter, quarter)
+
+                    @pl.when(jnp.logical_not(first))
+                    def _():
+                        line_a(p, way, d, q, neighbour).wait_recv()
+                        part_a[d, rows] += zr_a[p, way, d, rows]
+                    line_a(p, way, d, q, neighbour).start()
             return inner
 
-        lax.fori_loop(0, nz, pass_on, 0)
-
-        arrivals = ((0, z > 0), (1, z < nz - 1))
-        for way, there in arrivals:
-            @pl.when(there)
-            def _():
-                line_b(p, way, z, z).wait_recv()
-                part_b[z] += zr_b[p, way, z]
+        early = (nz + 1) // 2
+        lax.fori_loop(0, early, pass_on, 0)
+        for level in levels:
+            line_b(p, level, level).wait_recv()
+            part_b[...] += zr_b[p, level].astype(jnp.float32)
         for other in others:
             cross_b(p, other, x).start()
-        collect_a(z)
-        for way, there in arrivals:
-            @pl.when(there)
-            def _():
-                line_a(p, way, z, z).wait_recv()
-                part_a[z, x] += zr_a[p, way, z]
+        lax.fori_loop(early, nz, pass_on, 0)
 
         alpha = jnp.where(k == 0, 1.0, 2.0).astype(jnp.float32)
         beta = jnp.where(k == 0, 0.0, 1.0).astype(jnp.float32)
@@ -245,20 +254,28 @@
             now = cur[span]
             moved = (1.0 - SHIFT) * now - inv_ref[span] * summed
             following = alpha * moved - beta * prev[span]
+
+            @pl.when(k < ORDER - 1)
+            def _():
+                share(1 - p, part, inv_ref[span] * following)
             prev[span] = now
             cur[span] = following
             out_ref[span] = out_ref[span] + weight * following
 
-            @pl.when(k < ORDER - 1)
-            def _():
-                share(1 - p, part, inv_ref[span] * following)
-
-        finish(0, part_a[z, x])
-        summed = part_b[z, x]
+        summed = part_b[x]
         for other in others:
             cross_b(p, other, other).wait_recv()
             summed = summed + rx_b[p, other]
         finish(1, summed)
+        collect_a(z)
+        for way, there in ((0, z > 0), (1, z < nz - 1)):
+            @pl.when(there)
+            def _():
+                for q in range(PIECES):
+                    rows = pl.ds(q * quarter, quarter)
+                    line_a(p, way, z, q, z).wait_recv()
+                    part_a[z, rows] += zr_a[p, way, z, rows]
+        finish(0, part_a[z])
 
         for other in others:
             cross_b(p, other, x).wait_send()
@@ -270,8 +287,9 @@
 
             @pl.when(d != z)
             def _():
-                line_a(p, way, d, neighbour).wait_send()
-                line_b(p, way, d, neighbour).wait_send()
+                line_b(p, d, z).wait_send()
+                for q in range(PIECES):
+                    line_a(p, way, d, q, neighbour).wait_send()
             return inner
 
         lax.fori_loop(0, nz, drain, 0)
@@ -321,22 +339,25 @@
         return pl.pallas_call(
             functools.partial(filter_kernel, nz, nx, n_col),
             out_shape=jax.ShapeDtypeStruct((piece, width), f32),
-            in_specs=[smem, vmem, vmem, vmem, vmem],
+            in_specs=[smem, vmem, vmem, anywhere, anywhere],
             out_specs=vmem,
             scratch_shapes=[
+                pltpu.VMEM((2, n_row, block, n_col * block), jnp.bfloat16),
                 pltpu.VMEM((piece, width), f32),
                 pltpu.VMEM((piece, width), f32),
                 pltpu.VMEM((2, n_col * piece, width), jnp.bfloat16),
-                pltpu.VMEM((nz, nx, half, width), f32),
-                pltpu.VMEM((nz, nx, half, width), f32),
-                pltpu.VMEM((2, nz, nx, half, width), f32),
+                pltpu.VMEM((nz, half, width), f32),
+                pltpu.VMEM((nx, half, width), f32),
+                pltpu.VMEM((nz, nx, half, width), jnp.bfloat16),
+                pltpu.VMEM((nz, nx, half, width), jnp.bfloat16),
+                pltpu.VMEM((2, nz, nx, half, width), jnp.bfloat16),
                 pltpu.VMEM((2, nx, half, width), f32),
                 pltpu.VMEM((2, 2, nz, half, width), f32),
-                pltpu.VMEM((2, 2, nz, nx, half, width), f32),
-                dma((2, n_col)), dma((2, 2, n_col)),
+                pltpu.VMEM((2, nz, nx, half, width), jnp.bfloat16),
+                dma((2, n_row)), dma((2, n_col)), dma((2, 2, n_col)),
                 dma((nz, nx)), dma((2, nz, nx)),
-                dma((nz,)), dma((2, 2, nz)),
-                dma((nz,)), dma((2, 2, nz)),
+                dma((nz, PIECES)), dma((2, 2, nz, PIECES)),
+                dma((nz,)), dma((2, nz)),
                 dma((nx,)), dma((2, nx)),
             ],
             compiler_params=pltpu.CompilerParams(

time: 179 us -> 132 us (0.74)
  Pallas kernels: 175 us -> 127 us
    pallas_call x1, Pallas kernels: 167 us -> 118 us  [per_device(): pl.pallas_call(functools.partial(filter_kernel, nz, nx, n_col), out_shape...]
where the time goes in v2:
time: 132 us
  Pallas kernels  127 us (96%)
  local copies, waits for them, and re-layouts  3.78 us (3%)
    pallas_call x1, Pallas kernels, per_device(): pl.pallas_call(functools.partial(filter_kernel, nz, nx, n_col), out_shape...  118 us
    pallas_call x1, Pallas kernels, per_device(): pl.pallas_call(functools.partial(merge_kernel, n_row, n_col), out_shape=(...  8.62 us

profile of v2, /device:TPU:0, one launch (start us, length us, event | category | flops | bytes accessed | tf_op | source)
XLA Modules:
  0.0 131.7 jit_solution(11504792023265116233)
XLA Ops:
  0.7 0.7 convert_rsqrt_fusion
  1.3 0.8 copy.7
  2.1 0.7 reshape.8.layout_ref
  2.8 0.8 broadcast_in_dim.2.inv_ref
  3.5 8.6 %shard_map.64 = (bf16[8,256,1024]{2,1,0:T(8,128)(2,1)}, bf16[8,256,1024]{2,1,0:T(8,128)(2,1)}) custom-call(s32[1]{0:T(128)} %bitcast.4.count_ref, s32[256]{0:T(256)} %reshape.8.layout_ref, bf16[128,256,256]{2,1,0:T(8,128)(2,1)} %bitcast.5), custom_call_target="tpu_custom_call" | custom-call | tf_op jit(solution)/shard_map/pallas_call | solution.py:323
  12.2 118.0 %shard_map.65 = f32[256,128]{1,0:T(8,128)} custom-call(f32[7]{0:T(128)} %coef_ref.1, f32[256,128]{1,0:T(8,128)} %emb_ref.1, f32[256,128]{1,0:T(8,128)} %broadcast_in_dim.2.inv_ref, bf16[8,256,1024]{2,1,0:T(8,128)(2,1)} %get-tuple-element.7.hi_ref, bf16[8,256,1024]{2,1,0:T(8,128)(2,1)} %get-tuple-element.8.lo_ref), custom_call_target="tpu_custom_call" | custom-call | tf_op jit(solution)/shard_map/pallas_call | solution.py:339
  130.2 1.6 %copy.10 = f32[256,128]{1,0:T(8,128)} copy(f32[256,128]{1,0:T(8,128)} %shard_map.65) | data formatting | bytes 262144

commit v3 on v2

--- a/solution.py
+++ b/solution.py
@@ -16,7 +16,7 @@
 VMEM_LIMIT = 60 * 1024 * 1024
 
 
-def merge_kernel(n_row, n_col, count_ref, layout_ref, tiles_ref, hi_ref, lo_ref,
+def merge_kernel(n_row, n_col, count_ref, place_ref, tiles_ref, hi_ref, lo_ref,
                  total, landed, stage, in_sem, out_sem):
     block = tiles_ref.shape[1]
     count = count_ref[0]
@@ -46,7 +46,7 @@
 
             @pl.when(number < count)
             def _():
-                place = layout_ref[2 * number] * n_col + layout_ref[2 * number + 1]
+                place = place_ref[number]
                 total[place] += landed[slot, inner].astype(jnp.float32)
 
         @pl.when(chunk + DEPTH < chunks)
@@ -195,7 +195,7 @@
                 value = (jnp.dot(weights[0, number], source, preferred_element_type=jnp.float32)
                          + jnp.dot(weights[1, number], source, preferred_element_type=jnp.float32))
                 if u < nx - 1:
-                    tx_a[d, other] = value[:half].astype(jnp.bfloat16)
+                    tx_a[d, other] = value[:half]
                     cross_a(p, d, other, x).start()
                 else:
                     part_a[d] = value[:half]
@@ -218,7 +218,7 @@
         def collect_a(d):
             for other in others:
                 cross_a(p, d, other, other).wait_recv()
-                part_a[d] += rx_a[p, d, other].astype(jnp.float32)
+                part_a[d] += rx_a[p, d, other]
 
         def pass_on(t, inner):
             d, way, neighbour, first = visit(t)
@@ -314,8 +314,10 @@
         block = tiles.shape[1]
         piece, width = embedding.shape
         half = piece // 2
-        inv = lax.rsqrt(degrees.astype(jnp.float32))[:, None]
-        inv = jnp.broadcast_to(inv, (piece, width))
+        wide = jnp.broadcast_to(degrees[:, None], (piece, width))
+        inv = lax.rsqrt(wide.astype(jnp.float32))
+        layout = tile_layout[0, 0]
+        places = layout[:, 0] * n_col + layout[:, 1]
         smem = pl.BlockSpec(memory_space=pltpu.SMEM)
         vmem = pl.BlockSpec(memory_space=pltpu.VMEM)
         anywhere = pl.BlockSpec(memory_space=pl.ANY)
@@ -333,7 +335,7 @@
                 pltpu.SemaphoreType.DMA((2, 2)),
             ],
             compiler_params=pltpu.CompilerParams(vmem_limit_bytes=VMEM_LIMIT),
-        )(tile_count.reshape(1), tile_layout.reshape(-1), tiles)
+        )(tile_count.reshape(1), places, tiles)
         dma = pltpu.SemaphoreType.DMA
         f32 = jnp.float32
         return pl.pallas_call(
@@ -348,9 +350,9 @@
                 pltpu.VMEM((2, n_col * piece, width), jnp.bfloat16),
                 pltpu.VMEM((nz, half, width), f32),
                 pltpu.VMEM((nx, half, width), f32),
+                pltpu.VMEM((nz, nx, half, width), f32),
                 pltpu.VMEM((nz, nx, half, width), jnp.bfloat16),
-                pltpu.VMEM((nz, nx, half, width), jnp.bfloat16),
-                pltpu.VMEM((2, nz, nx, half, width), jnp.bfloat16),
+                pltpu.VMEM((2, nz, nx, half, width), f32),
                 pltpu.VMEM((2, nx, half, width), f32),
                 pltpu.VMEM((2, 2, nz, half, width), f32),
                 pltpu.VMEM((2, nz, nx, half, width), jnp.bfloat16),

time: 132 us -> 132 us (level)
  local copies, waits for them, and re-layouts: 3.78 us -> 2.33 us
    pallas_call x1, Pallas kernels: 118 us -> 120 us  [per_device(): pl.pallas_call(functools.partial(filter_kernel, nz, nx, n_col), out_shape...]
where the time goes in v3:
time: 132 us; the launch traced here: 133 us
  Pallas kernels  128 us (97%)
  local copies, waits for them, and re-layouts  2.33 us (2%)
  other arithmetic  1.96 us (1%)
    pallas_call x1, Pallas kernels, per_device(): pl.pallas_call(functools.partial(filter_kernel, nz, nx, n_col), out_shape...  120 us
    pallas_call x1, Pallas kernels, per_device(): pl.pallas_call(functools.partial(merge_kernel, n_row, n_col), out_shape=(...  7.63 us

profile of v3, /device:TPU:0, one launch (start us, length us, event | category | flops | bytes accessed | tf_op | source)
XLA Modules:
  0.0 132.7 jit_solution(12783591620675868037)
XLA Ops:
  0.7 1.3 add_bitcast_fusion.place_ref
  1.9 0.7 convert_rsqrt_fusion
  2.6 0.8 broadcast_in_dim.2.inv_ref
  3.4 7.6 %shard_map.64 = (bf16[8,256,1024]{2,1,0:T(8,128)(2,1)}, bf16[8,256,1024]{2,1,0:T(8,128)(2,1)}) custom-call(s32[1]{0:T(128)} %bitcast.5.count_ref, s32[128]{0:T(128)} %add_bitcast_fusion.place_ref, bf16[128,256,256]{2,1,0:T(8,128)(2,1)} %bitcast.6), custom_call_target="tpu_custom_call" | custom-call | tf_op jit(solution)/shard_map/pallas_call | solution.py:325
  11.0 120.1 %shard_map.65 = f32[256,128]{1,0:T(8,128)} custom-call(f32[7]{0:T(128)} %coef_ref.1, f32[256,128]{1,0:T(8,128)} %emb_ref.1, f32[256,128]{1,0:T(8,128)} %broadcast_in_dim.2.inv_ref, bf16[8,256,1024]{2,1,0:T(8,128)(2,1)} %get-tuple-element.7.hi_ref, bf16[8,256,1024]{2,1,0:T(8,128)(2,1)} %get-tuple-element.8.lo_ref), custom_call_target="tpu_custom_call" | custom-call | tf_op jit(solution)/shard_map/pallas_call | solution.py:341
  131.1 1.6 %copy.9 = f32[256,128]{1,0:T(8,128)} copy(f32[256,128]{1,0:T(8,128)} %shard_map.65) | data formatting | bytes 262144
